TPU v7x, 128 devices: a whole 4x4x4 slice. The times are simulated.
128 devices in a mesh: dp: 16 (over y_hi, x, core), mp: 8 (over z, y_lo).
Axes of the slice: x: 4, y: 4 (y_hi: 2, y_lo: 2; y = y_hi * 2 + y_lo), z: 4, core: 2. Of those that a mesh axis runs over, the one named last changes fastest.
Arguments:
- hidden_states: bfloat16 [65536, 4096], P('dp', 'mp'), may hold values from -1 to 1
- factor_values: bfloat16 [65536, 128], P('dp', 'mp'), may hold values from 0.029907227 to 0.13964844
- class_ids: int32 [65536, 128], P('dp', 'mp'), may hold values from 0 to 128255, as said below
- centers: int32 [3], replicated, may hold values from 0 to 65535
Outputs:
- min_distance: float32 [65536], P(('dp', 'mp'))
- weight_means: float32 [3], replicated
Inputs may be any that keep to these rules, and one draw needn't show every extreme that they name: `centers`: each value is a sample index. `class_ids`: entries k * 16 to (k + 1) * 16 - 1 of a row hold distinct classes of the k-th of 8 equal ranges of the vocabulary.
All inputs are finite; a program needn't handle non-finite values.
Results may differ from a plain program's by a relative error of at most 0.00095.
Values may be sent and summed in bfloat16 or wider, within the bound.
No kernel may reach another device: no remote copies, remote signals or barrier semaphores. Data moves between devices by JAX's collectives and lax.ppermute only.
A program may use at most 64 MiB of HBM per device.

v0:
```python
import functools

import jax
import jax.numpy as jnp
from jax import lax
from jax.experimental import pallas as pl
from jax.experimental.pallas import tpu as pltpu
from jax.sharding import Mesh
from jax.sharding import PartitionSpec as P

K_LOC = 16
STEPS = 3
LANES = 128
MP = ("mp_0", "mp_1")
DP = ("dp_0", "dp_1", "dp_2")
DP_MP = ("dp_0", "dp_1", "dp_2", "mp_0", "mp_1")
VMEM = pltpu.VMEM
F32 = jnp.float32
BF16 = jnp.bfloat16


def led_by(size, first):
    return [(first + i) % size for i in range(size)]


def vspec():
    return pl.BlockSpec(memory_space=VMEM)


def params(mib):
    return pltpu.CompilerParams(vmem_limit_bytes=mib * 1024 * 1024)


def pick_kernel(centers, hid, val, ids, out, cbuf, hbuf, vbuf, ibuf, rows, csem, sem):
    rows_all = hid.shape[0]
    first = pltpu.make_async_copy(centers, cbuf, csem)
    first.start()
    me = lax.axis_index(DP)
    chunks = hid.shape[1] // LANES
    out[...] = jnp.zeros_like(out)
    rows[...] = jnp.zeros_like(rows)
    lane = lax.broadcasted_iota(jnp.int32, (K_LOC, LANES), 1)
    entry = lax.broadcasted_iota(jnp.int32, (K_LOC, LANES), 0)
    first.wait()
    mine = [cbuf[t] // rows_all == me for t in range(STEPS)]

    @pl.when(functools.reduce(jnp.logical_or, mine))
    def _():
        copies = []
        for t in range(STEPS):
            off = lax.rem(cbuf[t], rows_all)
            row8 = pl.multiple_of((off // 8) * 8, 8)
            col = pl.multiple_of((off // LANES) * LANES, LANES)
            copies.append(pltpu.make_async_copy(hid.at[pl.ds(row8, 8), :], hbuf.at[t], sem.at[t, 0]))
            copies.append(pltpu.make_async_copy(val.at[:, pl.ds(col, LANES)], vbuf.at[t], sem.at[t, 1]))
            copies.append(pltpu.make_async_copy(ids.at[:, pl.ds(col, LANES)], ibuf.at[t], sem.at[t, 2]))
        for c in copies:
            c.start()
        for c in copies:
            c.wait()
        for t in range(STEPS):
            off = lax.rem(cbuf[t], rows_all)
            blk = hbuf[t].astype(F32)
            srow = lax.broadcasted_iota(jnp.int32, blk.shape, 0)
            here = srow == jnp.where(mine[t], lax.rem(off, 8), 8)
            row = jnp.sum(jnp.where(here, blk, 0.0), axis=0, keepdims=True)
            for j in range(chunks):
                rows[t * chunks + j : t * chunks + j + 1, :] = row[:, j * LANES : (j + 1) * LANES]
            here = lane == jnp.where(mine[t], lax.rem(off, LANES), LANES)
            vcol = jnp.sum(jnp.where(here, vbuf[t].astype(F32), 0.0), axis=1, keepdims=True)
            icol = jnp.sum(jnp.where(here, ibuf[t], 0), axis=1, keepdims=True)
            parts = (
                vcol,
                (icol >> 16).astype(F32),
                ((icol >> 8) & 255).astype(F32),
                (icol & 255).astype(F32),
            )
            spread = jnp.zeros((K_LOC, LANES), F32)
            for q, part in enumerate(parts):
                spread = jnp.where(lane == K_LOC * q + entry, part, spread)
            at = STEPS * chunks + t
            rows[at : at + 1, :] = jnp.sum(spread, axis=0, keepdims=True)
        tile = rows[...].astype(BF16)
        for d in range(out.shape[0]):
            out[d] = tile


def inner_kernel(first, got, hid, val, ids, out, cvec, idb, vb):
    n = out.shape[0]
    step = hid.shape[0] // n
    chunks = hid.shape[1] // LANES
    lane = lax.broadcasted_iota(jnp.int32, (K_LOC, LANES), 1)
    tile = got[0].astype(F32)
    for d in range(1, got.shape[0]):
        tile = tile + got[d].astype(F32)
    entry = lax.broadcasted_iota(jnp.int32, (K_LOC, LANES), 0)
    cvec[...] = jnp.zeros_like(cvec)
    norms = []
    for t in range(STEPS):
        for j in range(chunks):
            r = t * chunks + j
            cvec[2 + t : 3 + t, j * LANES : (j + 1) * LANES] = tile[r : r + 1, :]
        at = STEPS * chunks + t
        low = jnp.broadcast_to(tile[at : at + 1, :], (K_LOC, LANES))
        cs = [jnp.sum(jnp.where(lane == K_LOC * q + entry, low, 0.0), axis=1, keepdims=True) for q in range(4)]
        idc = (cs[1] * 65536.0 + cs[2] * 256.0 + cs[3]).astype(jnp.int32)
        for l in range(K_LOC):
            idb[t * K_LOC + l] = jnp.broadcast_to(idc[l : l + 1, :], (K_LOC, LANES)).astype(jnp.int16)
            vb[t * K_LOC + l] = jnp.broadcast_to(cs[0][l : l + 1, :], (K_LOC, LANES)).astype(BF16)
        norms.append(jnp.sum(cs[0] * cs[0], axis=0, keepdims=True))
    cmat = cvec[...]
    crow = lax.broadcasted_iota(jnp.int32, (8, LANES), 0)
    tail = jnp.broadcast_to(jnp.sum(cmat * cmat, axis=1, keepdims=True), (8, LANES))
    for t in range(STEPS):
        tail = jnp.where(crow == 2 + STEPS + t, norms[t], tail)
    cb = cmat.astype(BF16)
    srow = lax.broadcasted_iota(jnp.int32, (8, step), 0)
    dims = (((1,), (1,)), ((), ()))
    tiles = step // LANES
    for d in range(n):
        part = slice(d * step, (d + 1) * step)
        acc = lax.dot_general(cb, hid[part, :], dims, preferred_element_type=F32)
        total = None
        for j in range(chunks):
            h = hid[part, j * LANES : (j + 1) * LANES].astype(F32)
            total = h * h if total is None else total + h * h
        squares = [jnp.sum(total[k * LANES : (k + 1) * LANES, :].T, axis=0, keepdims=True) for k in range(tiles)]
        acc = jnp.where(srow == 0, jnp.concatenate(squares, axis=1), acc)
        ident = ids[:, part].astype(jnp.int16)
        vals = val[:, part].astype(F32)
        acc = jnp.where(srow == 1, jnp.sum(vals * vals, axis=0, keepdims=True), acc)
        for t in range(STEPS):
            w = [jnp.zeros((K_LOC, LANES), BF16)] * tiles
            for l in range(K_LOC):
                idl = idb[t * K_LOC + l]
                vl = vb[t * K_LOC + l]
                w = [jnp.where(ident[:, k * LANES : (k + 1) * LANES] == idl, vl, w[k]) for k in range(tiles)]
            w = jnp.concatenate(w, axis=1)
            aa = jnp.sum(w.astype(F32) * vals, axis=0, keepdims=True)
            acc = jnp.where(srow == 2 + STEPS + t, aa, acc)
        slot = (d - first) % n
        out[slot, :, 0:step] = acc
        out[slot, :, step:] = tail


def dist_kernel(parts, mind, sums):
    step = mind.shape[1]
    s = parts[0]
    for d in range(1, parts.shape[0]):
        s = s + parts[d]
    sq = s[0:1, 0:step] * s[1:2, 0:step]
    lane = lax.broadcasted_iota(jnp.int32, (1, LANES), 1)
    row = jnp.zeros((1, LANES), F32)
    low = None
    for t in range(STEPS):
        a, b = 2 + t, 2 + STEPS + t
        norm = s[a : a + 1, step : step + 1] * s[b : b + 1, step : step + 1]
        dist = sq + norm - 2.0 * s[a : a + 1, 0:step] * s[b : b + 1, 0:step]
        dist = jnp.maximum(dist, 0.0)
        low = dist if t == 0 else jnp.minimum(low, dist)
        row = jnp.where(lane == t, jnp.sum(low, axis=1, keepdims=True), row)
    mind[...] = low
    sums[...] = jnp.broadcast_to(row, sums.shape)


def pair_kernel(own, other, sums):
    sums[...] = jnp.broadcast_to(own[0:1, :] + other[0:1, :], sums.shape)


def mean_kernel(pool, sums, mind, out, low):
    low[...] = mind[...]
    total = jnp.sum(sums[...], axis=0) / pool
    out[...] = total[0 : out.shape[0]]


def body(hidden_states, factor_values, class_ids, centers):
    rows_all, width = hidden_states.shape
    n_dp, n_mp = lax.axis_size(DP), lax.axis_size(MP)
    n_all = n_dp * n_mp
    rows = rows_all // n_mp
    val = factor_values.T
    ids = class_ids.T
    first = 6
    hbm = pl.BlockSpec(memory_space=pltpu.HBM)

    picked = pl.pallas_call(
        pick_kernel,
        out_shape=jax.ShapeDtypeStruct((n_dp, 16, LANES), BF16),
        in_specs=[hbm] * 4,
        out_specs=vspec(),
        scratch_shapes=[
            pltpu.SMEM((STEPS,), jnp.int32),
            VMEM((STEPS, 8, width), BF16),
            VMEM((STEPS, K_LOC, LANES), BF16),
            VMEM((STEPS, K_LOC, LANES), jnp.int32),
            VMEM((16, LANES), F32),
            pltpu.SemaphoreType.DMA,
            pltpu.SemaphoreType.DMA((STEPS, 3)),
        ],
        compiler_params=params(4),
    )(*(pltpu.with_memory_space_constraint(x, pltpu.HBM) for x in (centers, hidden_states, val, ids)))
    got = lax.all_to_all(picked, DP, 0, 0, tiled=True, axis_index_groups=[led_by(n_dp, 13)])

    parts = pl.pallas_call(
        functools.partial(inner_kernel, first),
        out_shape=jax.ShapeDtypeStruct((n_mp, 8, rows + LANES), F32),
        in_specs=[vspec()] * 4,
        out_specs=vspec(),
        scratch_shapes=[
            VMEM((8, width), F32),
            VMEM((STEPS * K_LOC, K_LOC, LANES), jnp.int16),
            VMEM((STEPS * K_LOC, K_LOC, LANES), BF16),
        ],
        compiler_params=params(24),
    )(got, hidden_states, val, ids)
    parts = lax.all_to_all(parts, MP, 0, 0, tiled=True, axis_index_groups=[led_by(n_mp, first)])

    mind, sums = pl.pallas_call(
        dist_kernel,
        out_shape=[
            VMEM((1, rows), F32),
            jax.ShapeDtypeStruct((1, LANES), F32),
        ],
        in_specs=[vspec()],
        out_specs=[vspec(), vspec()],
        compiler_params=params(4),
    )(parts)
    other = lax.ppermute(sums, "dp_2", [(0, 1), (1, 0)])
    sums = pl.pallas_call(
        pair_kernel,
        out_shape=jax.ShapeDtypeStruct((n_all // 2, LANES), F32),
        in_specs=[vspec(), vspec()],
        out_specs=vspec(),
        compiler_params=params(4),
    )(sums, other)
    sums = lax.all_to_all(sums, ("dp_0", "dp_1", "mp_0", "mp_1"), 0, 0, tiled=True, axis_index_groups=[led_by(n_all // 2, 52)])
    means, mind = pl.pallas_call(
        functools.partial(mean_kernel, rows_all * n_dp),
        out_shape=[jax.ShapeDtypeStruct((STEPS,), F32), jax.ShapeDtypeStruct((1, rows), F32)],
        in_specs=[vspec(), vspec()],
        out_specs=[vspec(), vspec()],
        compiler_params=params(4),
    )(sums, mind)
    return mind.reshape(rows), means


def solution(mesh):
    finer = Mesh(mesh.devices.reshape(2, 4, 2, 4, 2), DP_MP)
    return jax.shard_map(
        body,
        mesh=finer,
        in_specs=(P(DP, MP), P(DP, MP), P(DP, MP), P()),
        out_specs=(P(DP_MP), P()),
        check_vma=False,
    )
```

profile of v0, /device:TPU:0, one launch (start us, length us, event | category | flops | bytes accessed | tf_op | source)
XLA Modules:
  0.0 41.7 jit_solution(5535620147707776936)
XLA Ops:
  0.6 0.0 copy-start
  0.6 0.0 copy-start.1
  0.7 0.0 copy-start.2
  0.7 0.9 %shard_map.59 = bf16[16,16,128]{2,1,0:T(8,128)(2,1)S(1)} custom-call(s32[3]{0:T(128)} %centers.1, bf16[4096,512]{1,0:T(8,128)(2,1)} %hid.3, bf16[16,4096]{1,0:T(8,128)(2,1)} %bitcast.9, s32[16,4096]{1,0:T(8,128)} %bitcast.7), custom_call_target="tpu_custom_call" | custom-call | tf_op jit(solution)/shard_map/pallas_call | solution.py:186
  1.6 11.5 %all_to_all.21.got = bf16[16,16,128]{2,1,0:T(8,128)(2,1)S(1)} all-to-all(bf16[16,16,128]{2,1,0:T(8,128)(2,1)S(1)} %shard_map.59), channel_id=1, replica_groups={{104,112,120,0,8,16,24,32,40,48,56,64,72,80,88,96},{105,113,121,1,9,17,..., dimensions={0} | all-to-all | bytes 131072 | tf_op jit(solution)/shard_map/all_to_all | solution.py:202
  13.1 0.0 copy-done
  13.1 0.0 copy-done.1
  13.1 0.0 copy-done.2
  13.1 1.6 %shard_map.60 = f32[8,8,640]{2,1,0:T(8,128)S(1)} custom-call(bf16[16,16,128]{2,1,0:T(8,128)(2,1)S(1)} %all_to_all.21.got, bf16[4096,512]{1,0:T(8,128)(2,1)S(1)} %copy-done, bf16[16,4096]{1,0:T(8,128)(2,1)S(1)} %bitcast.10, s32[16,4096]{1,0:T(8,128)S(1)} %bitcast.8), custom_call_target="tpu_custom_call" | custom-call | tf_op jit(solution)/shard_map/pallas_call | solution.py:204
  14.6 11.2 %all_to_all.22.parts = f32[8,8,640]{2,1,0:T(8,128)S(1)} all-to-all(f32[8,8,640]{2,1,0:T(8,128)S(1)} %shard_map.60), channel_id=1, replica_groups={{6,7,0,1,2,3,4,5},{14,15,8,9,10,11,12,13},{22,23,16,17,18,19,20,21},{30..., dimensions={0} | all-to-all | bytes 327680 | tf_op jit(solution)/shard_map/all_to_all | solution.py:216
  25.9 0.2 shard_map.61
  26.0 0.0 collective-permute-start
  26.0 1.1 %collective-permute-done.other = f32[1,128]{1,0:T(1,128)S(1)} collective-permute-done((f32[1,128]{1,0:T(1,128)S(1)}, f32[1,128]{1,0:T(1,128)S(1)}, u32[]{:S(2)}, u32[]{:S(2)}) %collective-permute-start) | collective-permute-done | bytes 544 | tf_op jit(solution)/shard_map/ppermute | solution.py:228
  27.2 13.9 %all_to_all.23 = f32[64,1,128]{2,1,0:T(1,128)S(1)} all-to-all(f32[64,1,128]{2,1,0:T(1,128)S(1)} %bitcast.12), channel_id=1, replica_groups={{100,101,102,103,112,113,114,115,116,117,118,119,0,1,2,3,4,5,6,7,16,17,..., dimensions={0} | all-to-all | bytes 65536 | tf_op jit(solution)/shard_map/all_to_all | solution.py:236
  41.1 0.6 %shard_map.63 = (f32[3]{0:T(128)}, f32[1,512]{1,0:T(1,128)}) custom-call(f32[64,128]{1,0:T(8,128)S(1)} %bitcast.11, f32[1,512]{1,0:T(1,128)S(1)} %get-tuple-element.7.mind), custom_call_target="tpu_custom_call" | custom-call | tf_op jit(solution)/shard_map/pallas_call | solution.py:237
  (1 shorter events, 0.0 us)
Async XLA Ops:
  0.6 12.4 %copy-start = (bf16[4096,512]{1,0:T(8,128)(2,1)S(1)}, bf16[4096,512]{1,0:T(8,128)(2,1)}, u32[]{:S(2)}) copy-start(bf16[4096,512]{1,0:T(8,128)(2,1)} %hid.3) | copy-start | bytes 12582916
  0.6 12.4 %copy-start.1 = (s32[4096,16]{0,1:T(8,128)S(1)}, s32[4096,16]{0,1:T(8,128)}, u32[]{:S(2)}) copy-start(s32[4096,16]{0,1:T(8,128)} %param.6) | copy-start | bytes 786436
  0.7 12.4 %copy-start.2 = (bf16[4096,16]{0,1:T(8,128)(2,1)S(1)}, bf16[4096,16]{0,1:T(8,128)(2,1)}, u32[]{:S(2)}) copy-start(bf16[4096,16]{0,1:T(8,128)(2,1)} %param.5) | copy-start | bytes 393220
  26.0 1.2 %collective-permute-start = (f32[1,128]{1,0:T(1,128)S(1)}, f32[1,128]{1,0:T(1,128)S(1)}, u32[]{:S(2)}, u32[]{:S(2)}) collective-permute-start(f32[1,128]{1,0:T(1,128)S(1)} %get-tuple-element.6.own), channel_id=1, source_target_pairs={{0,8},{8,0},{1,9},{9,1},{2,10},{10,2},{3,11},{11,3},{4,12},{12,4},... | collective-permute-start | bytes 1544 | tf_op jit(solution)/shard_map/ppermute | solution.py:228
where the time goes:
time: 41.6 us; the launch traced here: 41.7 us
  blocking collectives  36.6 us (88%)
  Pallas kernels  3.22 us (8%)
  waiting for transfers between devices  1.15 us (3%)
  between operations  0.68 us (2%)
    all_to_all x1, blocking collectives, body(): lax.all_to_all(sums, ('dp_0', 'dp_1', 'mp_0', 'mp_1'), 0, 0, tiled=True,...  13.9 us
    all_to_all x1, blocking collectives, body(): lax.all_to_all(picked, DP, 0, 0, tiled=True, axis_index_groups=[led_by(n_...  11.5 us
    all_to_all x1, blocking collectives, body(): lax.all_to_all(parts, MP, 0, 0, tiled=True, axis_index_groups=[led_by(n_m...  11.2 us
    pallas_call x1, Pallas kernels, body(): pl.pallas_call(functools.partial(inner_kernel, first), out_shape=jax.Shap...  1.56 us
    ppermute x1, waiting for transfers between devices, body(): other = lax.ppermute(sums, 'dp_2', [(0, 1), (1, 0)])  1.15 us
    pallas_call x1, Pallas kernels, body(): pl.pallas_call(pick_kernel, out_shape=jax.ShapeDtypeStruct((n_dp, 16, LAN...  0.91 us
  transfers between devices with their start and end apart: 1, of which 1 were waited for; matrix products, arithmetic and copies ran while one was open for 0% of the time, Pallas kernels for 0%

commit v1 on v0

--- a/solution.py
+++ b/solution.py
@@ -44,29 +44,36 @@
     first.wait()
     mine = [cbuf[t] // rows_all == me for t in range(STEPS)]
 
-    @pl.when(functools.reduce(jnp.logical_or, mine))
-    def _():
-        copies = []
-        for t in range(STEPS):
-            off = lax.rem(cbuf[t], rows_all)
-            row8 = pl.multiple_of((off // 8) * 8, 8)
-            col = pl.multiple_of((off // LANES) * LANES, LANES)
-            copies.append(pltpu.make_async_copy(hid.at[pl.ds(row8, 8), :], hbuf.at[t], sem.at[t, 0]))
-            copies.append(pltpu.make_async_copy(val.at[:, pl.ds(col, LANES)], vbuf.at[t], sem.at[t, 1]))
-            copies.append(pltpu.make_async_copy(ids.at[:, pl.ds(col, LANES)], ibuf.at[t], sem.at[t, 2]))
-        for c in copies:
-            c.start()
-        for c in copies:
-            c.wait()
-        for t in range(STEPS):
+    def copies(t):
+        off = lax.rem(cbuf[t], rows_all)
+        row8 = pl.multiple_of((off // 8) * 8, 8)
+        col = pl.multiple_of((off // LANES) * LANES, LANES)
+        return (
+            pltpu.make_async_copy(hid.at[pl.ds(row8, 8), :], hbuf.at[t], sem.at[t, 0]),
+            pltpu.make_async_copy(val.at[:, pl.ds(col, LANES)], vbuf.at[t], sem.at[t, 1]),
+            pltpu.make_async_copy(ids.at[:, pl.ds(col, LANES)], ibuf.at[t], sem.at[t, 2]),
+        )
+
+    for t in range(STEPS):
+
+        @pl.when(mine[t])
+        def _(t=t):
+            for c in copies(t):
+                c.start()
+
+    for t in range(STEPS):
+
+        @pl.when(mine[t])
+        def _(t=t):
+            for c in copies(t):
+                c.wait()
             off = lax.rem(cbuf[t], rows_all)
             blk = hbuf[t].astype(F32)
-            srow = lax.broadcasted_iota(jnp.int32, blk.shape, 0)
-            here = srow == jnp.where(mine[t], lax.rem(off, 8), 8)
+            here = lax.broadcasted_iota(jnp.int32, blk.shape, 0) == lax.rem(off, 8)
             row = jnp.sum(jnp.where(here, blk, 0.0), axis=0, keepdims=True)
             for j in range(chunks):
                 rows[t * chunks + j : t * chunks + j + 1, :] = row[:, j * LANES : (j + 1) * LANES]
-            here = lane == jnp.where(mine[t], lax.rem(off, LANES), LANES)
+            here = lane == lax.rem(off, LANES)
             vcol = jnp.sum(jnp.where(here, vbuf[t].astype(F32), 0.0), axis=1, keepdims=True)
             icol = jnp.sum(jnp.where(here, ibuf[t], 0), axis=1, keepdims=True)
             parts = (
@@ -80,6 +87,9 @@
                 spread = jnp.where(lane == K_LOC * q + entry, part, spread)
             at = STEPS * chunks + t
             rows[at : at + 1, :] = jnp.sum(spread, axis=0, keepdims=True)
+
+    @pl.when(functools.reduce(jnp.logical_or, mine))
+    def _():
         tile = rows[...].astype(BF16)
         for d in range(out.shape[0]):
             out[d] = tile

time: 41.6 us -> 41.2 us (level)
  blocking collectives: 36.6 us -> 35.9 us
    all_to_all x1, blocking collectives: 11.5 us -> 10.7 us  [body(): lax.all_to_all(picked, DP, 0, 0, tiled=True, axis_index_groups=[led_by(n_...]
where the time goes in v1:
time: 41.2 us; the launch traced here: 41 us
  blocking collectives  35.9 us (87%)
  Pallas kernels  3.27 us (8%)
  waiting for transfers between devices  1.15 us (3%)
  between operations  0.68 us (2%)
    all_to_all x1, blocking collectives, body(): lax.all_to_all(sums, ('dp_0', 'dp_1', 'mp_0', 'mp_1'), 0, 0, tiled=True,...  13.9 us
    all_to_all x1, blocking collectives, body(): lax.all_to_all(parts, MP, 0, 0, tiled=True, axis_index_groups=[led_by(n_m...  11.2 us
    all_to_all x1, blocking collectives, body(): lax.all_to_all(picked, DP, 0, 0, tiled=True, axis_index_groups=[led_by(n_...  10.7 us
    pallas_call x1, Pallas kernels, body(): pl.pallas_call(functools.partial(inner_kernel, first), out_shape=jax.Shap...  1.56 us
    ppermute x1, waiting for transfers between devices, body(): other = lax.ppermute(sums, 'dp_2', [(0, 1), (1, 0)])  1.15 us
    pallas_call x1, Pallas kernels, body(): pl.pallas_call(pick_kernel, out_shape=jax.ShapeDtypeStruct((n_dp, 16, LAN...  0.95 us
  transfers between devices with their start and end apart: 1, of which 1 were waited for; matrix products, arithmetic and copies ran while one was open for 0% of the time, Pallas kernels for 0%

profile of v1, /device:TPU:0, one launch (start us, length us, event | category | flops | bytes accessed | tf_op | source)
XLA Modules:
  0.0 41.0 jit_solution(3977030022330287078)
XLA Ops:
  0.6 0.0 copy-start
  0.6 0.0 copy-start.1
  0.7 0.0 copy-start.2
  0.7 1.0 %shard_map.59 = bf16[16,16,128]{2,1,0:T(8,128)(2,1)S(1)} custom-call(s32[3]{0:T(128)} %centers.1, bf16[4096,512]{1,0:T(8,128)(2,1)} %hid.3, bf16[16,4096]{1,0:T(8,128)(2,1)} %bitcast.9, s32[16,4096]{1,0:T(8,128)} %bitcast.7), custom_call_target="tpu_custom_call" | custom-call | tf_op jit(solution)/shard_map/pallas_call | solution.py:196
  1.6 10.7 %all_to_all.21.got = bf16[16,16,128]{2,1,0:T(8,128)(2,1)S(1)} all-to-all(bf16[16,16,128]{2,1,0:T(8,128)(2,1)S(1)} %shard_map.59), channel_id=1, replica_groups={{104,112,120,0,8,16,24,32,40,48,56,64,72,80,88,96},{105,113,121,1,9,17,..., dimensions={0} | all-to-all | bytes 131072 | tf_op jit(solution)/shard_map/all_to_all | solution.py:212
  12.3 0.0 copy-done
  12.3 0.0 copy-done.1
  12.3 0.0 copy-done.2
  12.3 1.6 %shard_map.60 = f32[8,8,640]{2,1,0:T(8,128)S(1)} custom-call(bf16[16,16,128]{2,1,0:T(8,128)(2,1)S(1)} %all_to_all.21.got, bf16[4096,512]{1,0:T(8,128)(2,1)S(1)} %copy-done, bf16[16,4096]{1,0:T(8,128)(2,1)S(1)} %bitcast.10, s32[16,4096]{1,0:T(8,128)S(1)} %bitcast.8), custom_call_target="tpu_custom_call" | custom-call | tf_op jit(solution)/shard_map/pallas_call | solution.py:214
  13.9 11.2 %all_to_all.22.parts = f32[8,8,640]{2,1,0:T(8,128)S(1)} all-to-all(f32[8,8,640]{2,1,0:T(8,128)S(1)} %shard_map.60), channel_id=1, replica_groups={{6,7,0,1,2,3,4,5},{14,15,8,9,10,11,12,13},{22,23,16,17,18,19,20,21},{30..., dimensions={0} | all-to-all | bytes 327680 | tf_op jit(solution)/shard_map/all_to_all | solution.py:226
  25.1 0.2 shard_map.61
  25.3 0.0 collective-permute-start
  25.3 1.1 %collective-permute-done.other = f32[1,128]{1,0:T(1,128)S(1)} collective-permute-done((f32[1,128]{1,0:T(1,128)S(1)}, f32[1,128]{1,0:T(1,128)S(1)}, u32[]{:S(2)}, u32[]{:S(2)}) %collective-permute-start) | collective-permute-done | bytes 544 | tf_op jit(solution)/shard_map/ppermute | solution.py:238
  26.5 13.9 %all_to_all.23 = f32[64,1,128]{2,1,0:T(1,128)S(1)} all-to-all(f32[64,1,128]{2,1,0:T(1,128)S(1)} %bitcast.12), channel_id=1, replica_groups={{100,101,102,103,112,113,114,115,116,117,118,119,0,1,2,3,4,5,6,7,16,17,..., dimensions={0} | all-to-all | bytes 65536 | tf_op jit(solution)/shard_map/all_to_all | solution.py:246
  40.4 0.6 %shard_map.63 = (f32[3]{0:T(128)}, f32[1,512]{1,0:T(1,128)}) custom-call(f32[64,128]{1,0:T(8,128)S(1)} %bitcast.11, f32[1,512]{1,0:T(1,128)S(1)} %get-tuple-element.7.mind), custom_call_target="tpu_custom_call" | custom-call | tf_op jit(solution)/shard_map/pallas_call | solution.py:247
  (1 shorter events, 0.0 us)
Async XLA Ops:
  0.6 11.7 %copy-start = (bf16[4096,512]{1,0:T(8,128)(2,1)S(1)}, bf16[4096,512]{1,0:T(8,128)(2,1)}, u32[]{:S(2)}) copy-start(bf16[4096,512]{1,0:T(8,128)(2,1)} %hid.3) | copy-start | bytes 12582916
  0.6 11.7 %copy-start.1 = (s32[4096,16]{0,1:T(8,128)S(1)}, s32[4096,16]{0,1:T(8,128)}, u32[]{:S(2)}) copy-start(s32[4096,16]{0,1:T(8,128)} %param.6) | copy-start | bytes 786436
  0.7 11.7 %copy-start.2 = (bf16[4096,16]{0,1:T(8,128)(2,1)S(1)}, bf16[4096,16]{0,1:T(8,128)(2,1)}, u32[]{:S(2)}) copy-start(bf16[4096,16]{0,1:T(8,128)(2,1)} %param.5) | copy-start | bytes 393220
  25.3 1.2 %collective-permute-start = (f32[1,128]{1,0:T(1,128)S(1)}, f32[1,128]{1,0:T(1,128)S(1)}, u32[]{:S(2)}, u32[]{:S(2)}) collective-permute-start(f32[1,128]{1,0:T(1,128)S(1)} %get-tuple-element.6.own), channel_id=1, source_target_pairs={{0,8},{8,0},{1,9},{9,1},{2,10},{10,2},{3,11},{11,3},{4,12},{12,4},... | collective-permute-start | bytes 1544 | tf_op jit(solution)/shard_map/ppermute | solution.py:238

commit v2 on v1

--- a/solution.py
+++ b/solution.py
@@ -54,42 +54,42 @@
             pltpu.make_async_copy(ids.at[:, pl.ds(col, LANES)], ibuf.at[t], sem.at[t, 2]),
         )
 
-    for t in range(STEPS):
-
-        @pl.when(mine[t])
-        def _(t=t):
-            for c in copies(t):
-                c.start()
-
-    for t in range(STEPS):
-
-        @pl.when(mine[t])
-        def _(t=t):
-            for c in copies(t):
-                c.wait()
-            off = lax.rem(cbuf[t], rows_all)
-            blk = hbuf[t].astype(F32)
-            here = lax.broadcasted_iota(jnp.int32, blk.shape, 0) == lax.rem(off, 8)
-            row = jnp.sum(jnp.where(here, blk, 0.0), axis=0, keepdims=True)
-            for j in range(chunks):
-                rows[t * chunks + j : t * chunks + j + 1, :] = row[:, j * LANES : (j + 1) * LANES]
-            here = lane == lax.rem(off, LANES)
-            vcol = jnp.sum(jnp.where(here, vbuf[t].astype(F32), 0.0), axis=1, keepdims=True)
-            icol = jnp.sum(jnp.where(here, ibuf[t], 0), axis=1, keepdims=True)
-            parts = (
-                vcol,
-                (icol >> 16).astype(F32),
-                ((icol >> 8) & 255).astype(F32),
-                (icol & 255).astype(F32),
-            )
-            spread = jnp.zeros((K_LOC, LANES), F32)
-            for q, part in enumerate(parts):
-                spread = jnp.where(lane == K_LOC * q + entry, part, spread)
-            at = STEPS * chunks + t
-            rows[at : at + 1, :] = jnp.sum(spread, axis=0, keepdims=True)
-
     @pl.when(functools.reduce(jnp.logical_or, mine))
     def _():
+        for t in range(STEPS):
+
+            @pl.when(mine[t])
+            def _(t=t):
+                for c in copies(t):
+                    c.start()
+
+        for t in range(STEPS):
+
+            @pl.when(mine[t])
+            def _(t=t):
+                for c in copies(t):
+                    c.wait()
+                off = lax.rem(cbuf[t], rows_all)
+                blk = hbuf[t].astype(F32)
+                here = lax.broadcasted_iota(jnp.int32, blk.shape, 0) == lax.rem(off, 8)
+                row = jnp.sum(jnp.where(here, blk, 0.0), axis=0, keepdims=True)
+                for j in range(chunks):
+                    rows[t * chunks + j : t * chunks + j + 1, :] = row[:, j * LANES : (j + 1) * LANES]
+                here = lane == lax.rem(off, LANES)
+                vcol = jnp.sum(jnp.where(here, vbuf[t].astype(F32), 0.0), axis=1, keepdims=True)
+                icol = jnp.sum(jnp.where(here, ibuf[t], 0), axis=1, keepdims=True)
+                parts = (
+                    vcol,
+                    (icol >> 16).astype(F32),
+                    ((icol >> 8) & 255).astype(F32),
+                    (icol & 255).astype(F32),
+                )
+                spread = jnp.zeros((K_LOC, LANES), F32)
+                for q, part in enumerate(parts):
+                    spread = jnp.where(lane == K_LOC * q + entry, part, spread)
+                at = STEPS * chunks + t
+                rows[at : at + 1, :] = jnp.sum(spread, axis=0, keepdims=True)
+
         tile = rows[...].astype(BF16)
         for d in range(out.shape[0]):
             out[d] = tile

time: 41.2 us -> 40.9 us (level)
  blocking collectives: 35.9 us -> 35.4 us
    all_to_all x1, blocking collectives: 13.9 us -> 13.4 us  [body(): lax.all_to_all(sums, ('dp_0', 'dp_1', 'mp_0', 'mp_1'), 0, 0, tiled=True,...]
where the time goes in v2:
time: 40.9 us; the launch traced here: 40.5 us
  blocking collectives  35.4 us (87%)
  Pallas kernels  3.22 us (8%)
  waiting for transfers between devices  1.15 us (3%)
  between operations  0.68 us (2%)
    all_to_all x1, blocking collectives, body(): lax.all_to_all(sums, ('dp_0', 'dp_1', 'mp_0', 'mp_1'), 0, 0, tiled=True,...  13.4 us
    all_to_all x1, blocking collectives, body(): lax.all_to_all(picked, DP, 0, 0, tiled=True, axis_index_groups=[led_by(n_...  11 us
    all_to_all x1, blocking collectives, body(): lax.all_to_all(parts, MP, 0, 0, tiled=True, axis_index_groups=[led_by(n_m...  11 us
    pallas_call x1, Pallas kernels, body(): pl.pallas_call(functools.partial(inner_kernel, first), out_shape=jax.Shap...  1.56 us
    ppermute x1, waiting for transfers between devices, body(): other = lax.ppermute(sums, 'dp_2', [(0, 1), (1, 0)])  1.15 us
    pallas_call x1, Pallas kernels, body(): pl.pallas_call(pick_kernel, out_shape=jax.ShapeDtypeStruct((n_dp, 16, LAN...  0.91 us
  transfers between devices with their start and end apart: 1, of which 1 were waited for; matrix products, arithmetic and copies ran while one was open for 0% of the time, Pallas kernels for 0%

profile of v2, /device:TPU:0, one launch (start us, length us, event | category | flops | bytes accessed | tf_op | source)
XLA Modules:
  0.0 40.5 jit_solution(13757832365780100155)
XLA Ops:
  0.6 0.0 copy-start
  0.6 0.0 copy-start.1
  0.7 0.0 copy-start.2
  0.7 0.9 %shard_map.59 = bf16[16,16,128]{2,1,0:T(8,128)(2,1)S(1)} custom-call(s32[3]{0:T(128)} %centers.1, bf16[4096,512]{1,0:T(8,128)(2,1)} %hid.3, bf16[16,4096]{1,0:T(8,128)(2,1)} %bitcast.9, s32[16,4096]{1,0:T(8,128)} %bitcast.7), custom_call_target="tpu_custom_call" | custom-call | tf_op jit(solution)/shard_map/pallas_call | solution.py:196
  1.6 11.0 %all_to_all.21.got = bf16[16,16,128]{2,1,0:T(8,128)(2,1)S(1)} all-to-all(bf16[16,16,128]{2,1,0:T(8,128)(2,1)S(1)} %shard_map.59), channel_id=1, replica_groups={{104,112,120,0,8,16,24,32,40,48,56,64,72,80,88,96},{105,113,121,1,9,17,..., dimensions={0} | all-to-all | bytes 131072 | tf_op jit(solution)/shard_map/all_to_all | solution.py:212
  12.6 0.0 copy-done
  12.6 0.0 copy-done.1
  12.6 0.0 copy-done.2
  12.6 1.6 %shard_map.60 = f32[8,8,640]{2,1,0:T(8,128)S(1)} custom-call(bf16[16,16,128]{2,1,0:T(8,128)(2,1)S(1)} %all_to_all.21.got, bf16[4096,512]{1,0:T(8,128)(2,1)S(1)} %copy-done, bf16[16,4096]{1,0:T(8,128)(2,1)S(1)} %bitcast.10, s32[16,4096]{1,0:T(8,128)S(1)} %bitcast.8), custom_call_target="tpu_custom_call" | custom-call | tf_op jit(solution)/shard_map/pallas_call | solution.py:214
  14.2 11.0 %all_to_all.22.parts = f32[8,8,640]{2,1,0:T(8,128)S(1)} all-to-all(f32[8,8,640]{2,1,0:T(8,128)S(1)} %shard_map.60), channel_id=1, replica_groups={{6,7,0,1,2,3,4,5},{14,15,8,9,10,11,12,13},{22,23,16,17,18,19,20,21},{30..., dimensions={0} | all-to-all | bytes 327680 | tf_op jit(solution)/shard_map/all_to_all | solution.py:226
  25.2 0.2 shard_map.61
  25.3 0.0 collective-permute-start
  25.4 1.1 %collective-permute-done.other = f32[1,128]{1,0:T(1,128)S(1)} collective-permute-done((f32[1,128]{1,0:T(1,128)S(1)}, f32[1,128]{1,0:T(1,128)S(1)}, u32[]{:S(2)}, u32[]{:S(2)}) %collective-permute-start) | collective-permute-done | bytes 544 | tf_op jit(solution)/shard_map/ppermute | solution.py:238
  26.5 13.4 %all_to_all.23 = f32[64,1,128]{2,1,0:T(1,128)S(1)} all-to-all(f32[64,1,128]{2,1,0:T(1,128)S(1)} %bitcast.12), channel_id=1, replica_groups={{100,101,102,103,112,113,114,115,116,117,118,119,0,1,2,3,4,5,6,7,16,17,..., dimensions={0} | all-to-all | bytes 65536 | tf_op jit(solution)/shard_map/all_to_all | solution.py:246
  39.9 0.6 %shard_map.63 = (f32[3]{0:T(128)}, f32[1,512]{1,0:T(1,128)}) custom-call(f32[64,128]{1,0:T(8,128)S(1)} %bitcast.11, f32[1,512]{1,0:T(1,128)S(1)} %get-tuple-element.7.mind), custom_call_target="tpu_custom_call" | custom-call | tf_op jit(solution)/shard_map/pallas_call | solution.py:247
  (1 shorter events, 0.0 us)
Async XLA Ops:
  0.6 12.0 %copy-start = (bf16[4096,512]{1,0:T(8,128)(2,1)S(1)}, bf16[4096,512]{1,0:T(8,128)(2,1)}, u32[]{:S(2)}) copy-start(bf16[4096,512]{1,0:T(8,128)(2,1)} %hid.3) | copy-start | bytes 12582916
  0.6 11.9 %copy-start.1 = (s32[4096,16]{0,1:T(8,128)S(1)}, s32[4096,16]{0,1:T(8,128)}, u32[]{:S(2)}) copy-start(s32[4096,16]{0,1:T(8,128)} %param.6) | copy-start | bytes 786436
  0.7 11.9 %copy-start.2 = (bf16[4096,16]{0,1:T(8,128)(2,1)S(1)}, bf16[4096,16]{0,1:T(8,128)(2,1)}, u32[]{:S(2)}) copy-start(bf16[4096,16]{0,1:T(8,128)(2,1)} %param.5) | copy-start | bytes 393220
  25.3 1.2 %collective-permute-start = (f32[1,128]{1,0:T(1,128)S(1)}, f32[1,128]{1,0:T(1,128)S(1)}, u32[]{:S(2)}, u32[]{:S(2)}) collective-permute-start(f32[1,128]{1,0:T(1,128)S(1)} %get-tuple-element.6.own), channel_id=1, source_target_pairs={{0,8},{8,0},{1,9},{9,1},{2,10},{10,2},{3,11},{11,3},{4,12},{12,4},... | collective-permute-start | bytes 1544 | tf_op jit(solution)/shard_map/ppermute | solution.py:238

commit v3 on v2

--- a/solution.py
+++ b/solution.py
@@ -95,7 +95,7 @@
             out[d] = tile
 
 
-def inner_kernel(first, got, hid, val, ids, out, cvec, idb, vb):
+def inner_kernel(order, got, hid, val, ids, out, cvec, idb, vb):
     n = out.shape[0]
     step = hid.shape[0] // n
     chunks = hid.shape[1] // LANES
@@ -148,7 +148,7 @@
             w = jnp.concatenate(w, axis=1)
             aa = jnp.sum(w.astype(F32) * vals, axis=0, keepdims=True)
             acc = jnp.where(srow == 2 + STEPS + t, aa, acc)
-        slot = (d - first) % n
+        slot = order.index(d)
         out[slot, :, 0:step] = acc
         out[slot, :, step:] = tail
 
@@ -190,7 +190,7 @@
     rows = rows_all // n_mp
     val = factor_values.T
     ids = class_ids.T
-    first = 6
+    order = [6, 4, 0, 2, 7, 5, 1, 3]
     hbm = pl.BlockSpec(memory_space=pltpu.HBM)
 
     picked = pl.pallas_call(
@@ -212,7 +212,7 @@
     got = lax.all_to_all(picked, DP, 0, 0, tiled=True, axis_index_groups=[led_by(n_dp, 13)])
 
     parts = pl.pallas_call(
-        functools.partial(inner_kernel, first),
+        functools.partial(inner_kernel, order),
         out_shape=jax.ShapeDtypeStruct((n_mp, 8, rows + LANES), F32),
         in_specs=[vspec()] * 4,
         out_specs=vspec(),
@@ -223,7 +223,7 @@
         ],
         compiler_params=params(24),
     )(got, hidden_states, val, ids)
-    parts = lax.all_to_all(parts, MP, 0, 0, tiled=True, axis_index_groups=[led_by(n_mp, first)])
+    parts = lax.all_to_all(parts, MP, 0, 0, tiled=True, axis_index_groups=[order])
 
     mind, sums = pl.pallas_call(
         dist_kernel,

time: 40.9 us -> 41.3 us (level)
  blocking collectives: 35.4 us -> 36 us
where the time goes in v3:
time: 41.3 us; the launch traced here: 41 us
  blocking collectives  36 us (87%)
  Pallas kernels  3.22 us (8%)
  waiting for transfers between devices  1.15 us (3%)
  between operations  0.68 us (2%)
    all_to_all x1, blocking collectives, body(): lax.all_to_all(sums, ('dp_0', 'dp_1', 'mp_0', 'mp_1'), 0, 0, tiled=True,...  13.7 us
    all_to_all x1, blocking collectives, body(): lax.all_to_all(parts, MP, 0, 0, tiled=True, axis_index_groups=[order])  11.3 us
    all_to_all x1, blocking collectives, body(): lax.all_to_all(picked, DP, 0, 0, tiled=True, axis_index_groups=[led_by(n_...  10.9 us
    pallas_call x1, Pallas kernels, body(): pl.pallas_call(functools.partial(inner_kernel, order), out_shape=jax.Shap...  1.56 us
    ppermute x1, waiting for transfers between devices, body(): other = lax.ppermute(sums, 'dp_2', [(0, 1), (1, 0)])  1.15 us
    pallas_call x1, Pallas kernels, body(): pl.pallas_call(pick_kernel, out_shape=jax.ShapeDtypeStruct((n_dp, 16, LAN...  0.91 us
  transfers between devices with their start and end apart: 1, of which 1 were waited for; matrix products, arithmetic and copies ran while one was open for 0% of the time, Pallas kernels for 0%

profile of v3, /device:TPU:0, one launch (start us, length us, event | category | flops | bytes accessed | tf_op | source)
XLA Modules:
  0.0 41.0 jit_solution(17353215078656267356)
XLA Ops:
  0.6 0.0 copy-start
  0.6 0.0 copy-start.1
  0.7 0.0 copy-start.2
  0.7 0.9 %shard_map.59 = bf16[16,16,128]{2,1,0:T(8,128)(2,1)S(1)} custom-call(s32[3]{0:T(128)} %centers.1, bf16[4096,512]{1,0:T(8,128)(2,1)} %hid.3, bf16[16,4096]{1,0:T(8,128)(2,1)} %bitcast.9, s32[16,4096]{1,0:T(8,128)} %bitcast.7), custom_call_target="tpu_custom_call" | custom-call | tf_op jit(solution)/shard_map/pallas_call | solution.py:196
  1.6 10.9 %all_to_all.21.got = bf16[16,16,128]{2,1,0:T(8,128)(2,1)S(1)} all-to-all(bf16[16,16,128]{2,1,0:T(8,128)(2,1)S(1)} %shard_map.59), channel_id=1, replica_groups={{104,112,120,0,8,16,24,32,40,48,56,64,72,80,88,96},{105,113,121,1,9,17,..., dimensions={0} | all-to-all | bytes 131072 | tf_op jit(solution)/shard_map/all_to_all | solution.py:212
  12.5 0.0 copy-done
  12.5 0.0 copy-done.1
  12.5 0.0 copy-done.2
  12.5 1.6 %shard_map.60 = f32[8,8,640]{2,1,0:T(8,128)S(1)} custom-call(bf16[16,16,128]{2,1,0:T(8,128)(2,1)S(1)} %all_to_all.21.got, bf16[4096,512]{1,0:T(8,128)(2,1)S(1)} %copy-done, bf16[16,4096]{1,0:T(8,128)(2,1)S(1)} %bitcast.10, s32[16,4096]{1,0:T(8,128)S(1)} %bitcast.8), custom_call_target="tpu_custom_call" | custom-call | tf_op jit(solution)/shard_map/pallas_call | solution.py:214
  14.1 11.3 %all_to_all.22.parts = f32[8,8,640]{2,1,0:T(8,128)S(1)} all-to-all(f32[8,8,640]{2,1,0:T(8,128)S(1)} %shard_map.60), channel_id=1, replica_groups={{6,4,0,2,7,5,1,3},{14,12,8,10,15,13,9,11},{22,20,16,18,23,21,17,19},{30..., dimensions={0} | all-to-all | bytes 327680 | tf_op jit(solution)/shard_map/all_to_all | solution.py:226
  25.4 0.2 shard_map.61
  25.6 0.0 collective-permute-start
  25.6 1.1 %collective-permute-done.other = f32[1,128]{1,0:T(1,128)S(1)} collective-permute-done((f32[1,128]{1,0:T(1,128)S(1)}, f32[1,128]{1,0:T(1,128)S(1)}, u32[]{:S(2)}, u32[]{:S(2)}) %collective-permute-start) | collective-permute-done | bytes 544 | tf_op jit(solution)/shard_map/ppermute | solution.py:238
  26.8 13.7 %all_to_all.23 = f32[64,1,128]{2,1,0:T(1,128)S(1)} all-to-all(f32[64,1,128]{2,1,0:T(1,128)S(1)} %bitcast.12), channel_id=1, replica_groups={{100,101,102,103,112,113,114,115,116,117,118,119,0,1,2,3,4,5,6,7,16,17,..., dimensions={0} | all-to-all | bytes 65536 | tf_op jit(solution)/shard_map/all_to_all | solution.py:246
  40.5 0.6 %shard_map.63 = (f32[3]{0:T(128)}, f32[1,512]{1,0:T(1,128)}) custom-call(f32[64,128]{1,0:T(8,128)S(1)} %bitcast.11, f32[1,512]{1,0:T(1,128)S(1)} %get-tuple-element.7.mind), custom_call_target="tpu_custom_call" | custom-call | tf_op jit(solution)/shard_map/pallas_call | solution.py:247
  (1 shorter events, 0.0 us)
Async XLA Ops:
  0.6 11.9 %copy-start = (bf16[4096,512]{1,0:T(8,128)(2,1)S(1)}, bf16[4096,512]{1,0:T(8,128)(2,1)}, u32[]{:S(2)}) copy-start(bf16[4096,512]{1,0:T(8,128)(2,1)} %hid.3) | copy-start | bytes 12582916
  0.6 11.9 %copy-start.1 = (s32[4096,16]{0,1:T(8,128)S(1)}, s32[4096,16]{0,1:T(8,128)}, u32[]{:S(2)}) copy-start(s32[4096,16]{0,1:T(8,128)} %param.6) | copy-start | bytes 786436
  0.7 11.9 %copy-start.2 = (bf16[4096,16]{0,1:T(8,128)(2,1)S(1)}, bf16[4096,16]{0,1:T(8,128)(2,1)}, u32[]{:S(2)}) copy-start(bf16[4096,16]{0,1:T(8,128)(2,1)} %param.5) | copy-start | bytes 393220
  25.6 1.2 %collective-permute-start = (f32[1,128]{1,0:T(1,128)S(1)}, f32[1,128]{1,0:T(1,128)S(1)}, u32[]{:S(2)}, u32[]{:S(2)}) collective-permute-start(f32[1,128]{1,0:T(1,128)S(1)} %get-tuple-element.6.own), channel_id=1, source_target_pairs={{0,8},{8,0},{1,9},{9,1},{2,10},{10,2},{3,11},{11,3},{4,12},{12,4},... | collective-permute-start | bytes 1544 | tf_op jit(solution)/shard_map/ppermute | solution.py:238

commit v4 on v3

--- a/solution.py
+++ b/solution.py
@@ -209,7 +209,7 @@
         ],
         compiler_params=params(4),
     )(*(pltpu.with_memory_space_constraint(x, pltpu.HBM) for x in (centers, hidden_states, val, ids)))
-    got = lax.all_to_all(picked, DP, 0, 0, tiled=True, axis_index_groups=[led_by(n_dp, 13)])
+    got = lax.all_to_all(picked, DP, 0, 0, tiled=True, axis_index_groups=[[13, 1, 0, 3, 2, 7, 6, 5, 4, 9, 8, 11, 10, 15, 14, 12]])
 
     parts = pl.pallas_call(
         functools.partial(inner_kernel, order),

time: 41.3 us -> 41.3 us (level)
    all_to_all x1, blocking collectives: 10.9 us -> 11.4 us  [body(): lax.all_to_all(picked, DP, 0, 0, tiled=True, axis_index_groups=[[13, 1, 0...]
where the time goes in v4:
time: 41.3 us; the launch traced here: 41.1 us
  blocking collectives  36 us (87%)
  Pallas kernels  3.22 us (8%)
  waiting for transfers between devices  1.15 us (3%)
  between operations  0.68 us (2%)
    all_to_all x1, blocking collectives, body(): lax.all_to_all(sums, ('dp_0', 'dp_1', 'mp_0', 'mp_1'), 0, 0, tiled=True,...  13.4 us
    all_to_all x1, blocking collectives, body(): lax.all_to_all(picked, DP, 0, 0, tiled=True, axis_index_groups=[[13, 1, 0...  11.4 us
    all_to_all x1, blocking collectives, body(): lax.all_to_all(parts, MP, 0, 0, tiled=True, axis_index_groups=[order])  11.2 us
    pallas_call x1, Pallas kernels, body(): pl.pallas_call(functools.partial(inner_kernel, order), out_shape=jax.Shap...  1.56 us
    ppermute x1, waiting for transfers between devices, body(): other = lax.ppermute(sums, 'dp_2', [(0, 1), (1, 0)])  1.15 us
    pallas_call x1, Pallas kernels, body(): pl.pallas_call(pick_kernel, out_shape=jax.ShapeDtypeStruct((n_dp, 16, LAN...  0.91 us
  transfers between devices with their start and end apart: 1, of which 1 were waited for; matrix products, arithmetic and copies ran while one was open for 0% of the time, Pallas kernels for 0%

profile of v4, /device:TPU:0, one launch (start us, length us, event | category | flops | bytes accessed | tf_op | source)
XLA Modules:
  0.0 41.1 jit_solution(9544397131919986908)
XLA Ops:
  0.6 0.0 copy-start
  0.6 0.0 copy-start.1
  0.7 0.0 copy-start.2
  0.7 0.9 %shard_map.59 = bf16[16,16,128]{2,1,0:T(8,128)(2,1)S(1)} custom-call(s32[3]{0:T(128)} %centers.1, bf16[4096,512]{1,0:T(8,128)(2,1)} %hid.3, bf16[16,4096]{1,0:T(8,128)(2,1)} %bitcast.9, s32[16,4096]{1,0:T(8,128)} %bitcast.7), custom_call_target="tpu_custom_call" | custom-call | tf_op jit(solution)/shard_map/pallas_call | solution.py:196
  1.6 11.4 %all_to_all.21.got = bf16[16,16,128]{2,1,0:T(8,128)(2,1)S(1)} all-to-all(bf16[16,16,128]{2,1,0:T(8,128)(2,1)S(1)} %shard_map.59), channel_id=1, replica_groups={{104,8,0,24,16,56,48,40,32,72,64,88,80,120,112,96},{105,9,1,25,17,57,49..., dimensions={0} | all-to-all | bytes 131072 | tf_op jit(solution)/shard_map/all_to_all | solution.py:212
  13.0 0.0 copy-done
  13.0 0.0 copy-done.1
  13.0 0.0 copy-done.2
  13.0 1.6 %shard_map.60 = f32[8,8,640]{2,1,0:T(8,128)S(1)} custom-call(bf16[16,16,128]{2,1,0:T(8,128)(2,1)S(1)} %all_to_all.21.got, bf16[4096,512]{1,0:T(8,128)(2,1)S(1)} %copy-done, bf16[16,4096]{1,0:T(8,128)(2,1)S(1)} %bitcast.10, s32[16,4096]{1,0:T(8,128)S(1)} %bitcast.8), custom_call_target="tpu_custom_call" | custom-call | tf_op jit(solution)/shard_map/pallas_call | solution.py:214
  14.6 11.2 %all_to_all.22.parts = f32[8,8,640]{2,1,0:T(8,128)S(1)} all-to-all(f32[8,8,640]{2,1,0:T(8,128)S(1)} %shard_map.60), channel_id=1, replica_groups={{6,4,0,2,7,5,1,3},{14,12,8,10,15,13,9,11},{22,20,16,18,23,21,17,19},{30..., dimensions={0} | all-to-all | bytes 327680 | tf_op jit(solution)/shard_map/all_to_all | solution.py:226
  25.8 0.2 shard_map.61
  25.9 0.0 collective-permute-start
  26.0 1.1 %collective-permute-done.other = f32[1,128]{1,0:T(1,128)S(1)} collective-permute-done((f32[1,128]{1,0:T(1,128)S(1)}, f32[1,128]{1,0:T(1,128)S(1)}, u32[]{:S(2)}, u32[]{:S(2)}) %collective-permute-start) | collective-permute-done | bytes 544 | tf_op jit(solution)/shard_map/ppermute | solution.py:238
  27.1 13.4 %all_to_all.23 = f32[64,1,128]{2,1,0:T(1,128)S(1)} all-to-all(f32[64,1,128]{2,1,0:T(1,128)S(1)} %bitcast.12), channel_id=1, replica_groups={{100,101,102,103,112,113,114,115,116,117,118,119,0,1,2,3,4,5,6,7,16,17,..., dimensions={0} | all-to-all | bytes 65536 | tf_op jit(solution)/shard_map/all_to_all | solution.py:246
  40.5 0.6 %shard_map.63 = (f32[3]{0:T(128)}, f32[1,512]{1,0:T(1,128)}) custom-call(f32[64,128]{1,0:T(8,128)S(1)} %bitcast.11, f32[1,512]{1,0:T(1,128)S(1)} %get-tuple-element.7.mind), custom_call_target="tpu_custom_call" | custom-call | tf_op jit(solution)/shard_map/pallas_call | solution.py:247
  (1 shorter events, 0.0 us)
Async XLA Ops:
  0.6 12.4 %copy-start = (bf16[4096,512]{1,0:T(8,128)(2,1)S(1)}, bf16[4096,512]{1,0:T(8,128)(2,1)}, u32[]{:S(2)}) copy-start(bf16[4096,512]{1,0:T(8,128)(2,1)} %hid.3) | copy-start | bytes 12582916
  0.6 12.3 %copy-start.1 = (s32[4096,16]{0,1:T(8,128)S(1)}, s32[4096,16]{0,1:T(8,128)}, u32[]{:S(2)}) copy-start(s32[4096,16]{0,1:T(8,128)} %param.6) | copy-start | bytes 786436
  0.7 12.3 %copy-start.2 = (bf16[4096,16]{0,1:T(8,128)(2,1)S(1)}, bf16[4096,16]{0,1:T(8,128)(2,1)}, u32[]{:S(2)}) copy-start(bf16[4096,16]{0,1:T(8,128)(2,1)} %param.5) | copy-start | bytes 393220
  25.9 1.2 %collective-permute-start = (f32[1,128]{1,0:T(1,128)S(1)}, f32[1,128]{1,0:T(1,128)S(1)}, u32[]{:S(2)}, u32[]{:S(2)}) collective-permute-start(f32[1,128]{1,0:T(1,128)S(1)} %get-tuple-element.6.own), channel_id=1, source_target_pairs={{0,8},{8,0},{1,9},{9,1},{2,10},{10,2},{3,11},{11,3},{4,12},{12,4},... | collective-permute-start | bytes 1544 | tf_op jit(solution)/shard_map/ppermute | solution.py:238
